TPU v7x, 32 devices: a whole 2x2x4 slice. The times are simulated.
32 devices in a mesh: high: 4 (over x, core), low: 8 (over z, y).
Axes of the slice: x: 2, y: 2, z: 4, core: 2. Of those that a mesh axis runs over, the one named last changes fastest.
Arguments:
- wave_parts: float32 [2, 512, 128, 128], P(None, ('high', 'low')), may hold values from -6 to 6
- level_table: float32 [512, 128, 128], P(('high', 'low')), may hold values from -2 to 2
- diagonal_angles: float32 [2, 128], replicated, may hold values from 0.3 to 1.2
- turn_angles: float32 [2, 4], replicated, may hold values from 0.3 to 1.2
Outputs:
- state_after: float32 [2, 512, 128, 128], P(None, ('high', 'low'))
All inputs are finite; a program needn't handle non-finite values.
Results may differ from a plain program's by a relative error of at most 0.0003.
Values sent between devices are 32-bit elements.
A program may use at most 64 MiB of HBM per device.

v0:
```python
import functools

import jax
import jax.numpy as jnp
import numpy as np
from jax import lax
from jax.experimental import pallas as pl
from jax.experimental.pallas import tpu as pltpu
from jax.sharding import PartitionSpec as P

MESH = pl.DeviceIdType.MESH
F32 = jnp.float32
BF16 = jnp.bfloat16


def fit(function, powers, reach=3.2):
    x = np.cos(np.pi * (np.arange(4000) + 0.5) / 4000) * reach
    scaled = np.stack([(x / reach) ** p for p in powers], 1)
    found = np.linalg.lstsq(scaled, function(x), rcond=None)[0]
    return [float(f / reach**p) for f, p in zip(found, powers)]


SIN = fit(np.sin, range(1, 16, 2))
COS = fit(np.cos, range(0, 17, 2))


def cos_sin(x):
    z = x * x
    sine = jnp.full_like(x, SIN[-1])
    for f in SIN[-2::-1]:
        sine = sine * z + f
    cosine = jnp.full_like(x, COS[-1])
    for f in COS[-2::-1]:
        cosine = cosine * z + f
    return cosine, sine * x


def bits_of(count):
    return count.bit_length() - 1


def pop(values, bits):
    total = values % 2
    for q in range(1, bits):
        total = total + (values // 2**q) % 2
    return total


def pop_array(values, bits):
    total = values & 1
    for q in range(1, bits):
        total = total + ((values >> q) & 1)
    return total


def mix_list(xs, turns):
    for q, (c, s) in enumerate(turns):
        step = 1 << q
        ys = list(xs)
        for i in range(len(xs)):
            if not i & step:
                u, v = xs[i], xs[i + step]
                ys[i] = c * u - s * v
                ys[i + step] = s * u + c * v
        xs = ys
    return xs


def rotation(count, c, s, transposed):
    i = lax.broadcasted_iota(jnp.int32, (count, count), 0)
    j = lax.broadcasted_iota(jnp.int32, (count, count), 1)
    if transposed:
        i, j = j, i
    c, s = c[:1, :count], s[:1, :count]
    table = jnp.ones((count, count), F32)
    for q in range(bits_of(count)):
        a, b = (i >> q) & 1, (j >> q) & 1
        table = table * jnp.where(a == b, c, jnp.where(a == 1, s, -s))
    return table


def split(x):
    hi = x.astype(BF16)
    return hi, (x - hi.astype(F32)).astype(BF16)


def kernel(nh, nl, parts, wave_hbm, level_hbm, diag_hbm, turn_hbm, out_hbm,
           out, out_sem, diag, turn, wave, level, abuf, recv, lev, back, home, lane_t, row_t,
           in_sem, lev_send, lev_recv, to_send, to_recv, ret_send, ret_recv):
    n = nh * nl
    blocks, rows, lanes = level.shape
    cut = n // blocks
    rp = rows // cut
    rq = rp // parts
    h, l = lax.axis_index("high"), lax.axis_index("low")
    me = h * nl + l

    def others(body):
        def step(k, carry):
            dh = lax.rem(h + k // nl, nh)
            dl = lax.rem(l + k % nl, nl)
            body(dh * nl + dl, (dh, dl))
            return carry
        lax.fori_loop(1, n, step, 0)

    level_in = pltpu.make_async_copy(level_hbm, level, in_sem.at[0])
    wave_in = pltpu.make_async_copy(wave_hbm, wave, in_sem.at[1])
    diag_in = pltpu.make_async_copy(diag_hbm, diag, in_sem.at[2])
    turn_in = pltpu.make_async_copy(turn_hbm, turn, in_sem.at[3])
    turn_in.start()
    diag_in.start()
    level_in.start()
    wave_in.start()

    barrier = pltpu.get_barrier_semaphore()
    others(lambda d, at: pl.semaphore_signal(barrier, inc=1, device_id=at, device_id_type=MESH))
    pl.semaphore_wait(barrier, n - 1)

    def own_rows(d):
        return pl.ds(pl.multiple_of((d % cut) * rp, 8), rp)

    def level_copy(d, at):
        return pltpu.make_async_remote_copy(
            src_ref=level_hbm.at[d // cut, own_rows(d)], dst_ref=lev.at[me],
            send_sem=lev_send.at[d], recv_sem=lev_recv.at[me],
            device_id=at, device_id_type=MESH)

    def to_copy(q):
        return lambda d, at: pltpu.make_async_remote_copy(
            src_ref=abuf.at[d, q], dst_ref=recv.at[me, q], send_sem=to_send.at[q, d],
            recv_sem=to_recv.at[q, me], device_id=at, device_id_type=MESH)

    def ret_copy(part, q):
        part_rows = pl.ds(q * rq, rq)
        return lambda d, at: pltpu.make_async_remote_copy(
            src_ref=back.at[d, part, part_rows], dst_ref=home.at[me, part, part_rows],
            send_sem=ret_send.at[part, q, d], recv_sem=ret_recv.at[part, q, me],
            device_id=at, device_id_type=MESH)

    def start_all(copy):
        others(lambda d, at: copy(d, at).start())

    def wait_all(block_of, sem):
        others(lambda d, at: pltpu.make_async_copy(block_of(d), block_of(d), sem.at[d]).wait())

    start_all(level_copy)

    turn_in.wait()
    diag_in.wait()

    turns = []
    for layer in range(2):
        turns.append([cos_sin(jnp.full((8, lanes), turn[layer, g], F32)) for g in range(4)])
        c, s = turns[layer][0]
        hi, lo = split(rotation(lanes, c, s, True))
        lane_t[layer] = jnp.concatenate(
            [jnp.concatenate([hi, lo], 1), jnp.concatenate([hi, jnp.zeros_like(hi)], 1)], 0)
        c, s = turns[layer][1]
        hi, lo = split(rotation(rows, c, s, False))
        row_t[layer] = jnp.concatenate(
            [jnp.concatenate([hi, hi], 1), jnp.concatenate([lo, jnp.zeros_like(hi)], 1)], 0)

    ones = pop_array(lax.broadcasted_iota(jnp.int32, (rows, lanes), 0), bits_of(rows)) + pop_array(
        lax.broadcasted_iota(jnp.int32, (rows, lanes), 1), bits_of(lanes))
    ones_dev = pop(me, bits_of(n))

    def mix_lanes(x, layer):
        hi, lo = split(x)
        z = jnp.dot(jnp.concatenate([hi, lo], 1), lane_t[layer], preferred_element_type=F32)
        return z[:, :lanes] + z[:, lanes:]

    def mix_rows(x, y, layer):
        hi, lo = split(jnp.concatenate([x, y], 1))
        z = jnp.dot(row_t[layer], jnp.concatenate([hi, lo], 0), preferred_element_type=F32)
        z = z[:rows] + z[rows:]
        return z[:, :lanes], z[:, lanes:]

    def mix_blocks(buf, middle_at, start, count, layer):
        pair = [turns[layer][2]] * bits_of(blocks)
        per = count // 8

        def body(t, carry):
            p, at = t // per, pl.ds(pl.multiple_of(start + (t % per) * 8, 8), 8)
            xs = mix_list([buf[b * cut + p, middle_at, at] for b in range(blocks)], pair)
            for b in range(blocks):
                buf[b * cut + p, middle_at, at] = xs[b]
            return carry
        lax.fori_loop(0, cut * per, body, 0)

    def quarter(b):
        k = (ones + (ones_dev + pop(b, bits_of(blocks)))) & 3
        return (k & 1) == 1, jnp.where(k >= 2, -1.0, 1.0)

    level_in.wait()
    wave_in.wait()
    lev[me] = level[me // cut, own_rows(me)]

    def first(b, carry):
        c, s = cos_sin(level[b] * diag[pl.ds(0, 1), :])
        odd, sign = quarter(b)
        cc = jnp.where(odd, s, c) * sign
        ss = jnp.where(odd, -c, s) * sign
        re, im = wave[0, b], wave[1, b]
        z = mix_lanes(jnp.concatenate([re * cc + im * ss, im * cc - re * ss], 0), 0)
        re, im = mix_rows(z[:rows], z[rows:], 0)
        for p in range(cut):
            for q in range(parts):
                at = p * rp + q * rq
                abuf[b * cut + p, q, :rq] = re[at:at + rq]
                abuf[b * cut + p, q, rq:] = im[at:at + rq]
        return carry
    lax.fori_loop(0, blocks, first, 0)
    for q in range(parts):
        mix_blocks(abuf, q, 0, 2 * rq, 0)
        start_all(to_copy(q))
        recv[me, q] = abuf[me, q]

    def dev_turns(layer):
        return [turns[layer][3]] * bits_of(nl) + [turns[layer][2]] * bits_of(nh)

    def middle(q):
        def body(j, carry):
            at = pl.ds(pl.multiple_of(j * 8, 8), 8)
            at_im = pl.ds(pl.multiple_of(rq + j * 8, 8), 8)
            at_part = pl.ds(pl.multiple_of(q * rq + j * 8, 8), 8)
            xs = mix_list([recv[d, q, at] for d in range(n)], dev_turns(0))
            for d in range(n):
                recv[d, q, at] = xs[d]
            ys = mix_list([recv[d, q, at_im] for d in range(n)], dev_turns(0))
            angle = diag[pl.ds(1, 1), :]
            for d in range(n):
                c, s = cos_sin(lev[d, at_part] * angle)
                x, y = recv[d, q, at], ys[d]
                recv[d, q, at] = x * c + y * s
                ys[d] = y * c - x * s
            ys = mix_list(ys, dev_turns(1))
            for d in range(n):
                back[d, 1, at_part] = ys[d]
            xs = mix_list([recv[d, q, at] for d in range(n)], dev_turns(1))
            for d in range(n):
                back[d, 0, at_part] = xs[d]
            return carry
        lax.fori_loop(0, rq // 8, body, 0)

    def middle_lanes(part, q):
        group = min(n, 256 // rq)
        at = pl.ds(q * rq, rq)
        for i in range(n // group):
            ds = pl.ds(i * group, group)
            z = mix_lanes(back[ds, part, at].reshape(group * rq, lanes), 1)
            back[ds, part, at] = z.reshape(group, rq, lanes)

    wait_all(lambda d: lev.at[d], lev_recv)
    for q in range(parts):
        wait_all(lambda d: recv.at[d, q], to_recv.at[q])
        middle(q)
        middle_lanes(0, q)
        start_all(ret_copy(0, q))
        middle_lanes(1, q)
    for q in range(parts):
        start_all(ret_copy(1, q))
    home[me] = back[me]

    def gather(b, part):
        return jnp.concatenate([home[b * cut + p, part] for p in range(cut)], 0)

    def out_copy(i):
        pair = pl.ds(2 * i, 2)
        return pltpu.make_async_copy(out.at[:, pair], out_hbm.at[:, pair], out_sem.at[i])

    for part in range(2):
        for q in range(parts):
            wait_all(lambda d: home.at[d, part, pl.ds(q * rq, rq)], ret_recv.at[part, q])
            mix_blocks(home, part, q * rq, rq, 1)

        def last(i, carry):
            b = 2 * i
            for at, x in zip((b, b + 1), mix_rows(gather(b, part), gather(b + 1, part), 1)):
                if part == 0:
                    wave[0, at] = x
                else:
                    odd, sign = quarter(at)
                    re = wave[0, at]
                    out[0, at] = jnp.where(odd, x, re) * sign
                    out[1, at] = jnp.where(odd, -re, x) * sign
            if part == 1:
                out_copy(i).start()
            return carry
        lax.fori_loop(0, blocks // 2, last, 0, unroll=4)

    def drain(d, at):
        level_copy(d, at).wait_send()
        for q in range(parts):
            to_copy(q)(d, at).wait_send()
            for part in range(2):
                ret_copy(part, q)(d, at).wait_send()
    others(drain)
    for i in range(blocks // 2):
        out_copy(i).wait()


def solution(mesh):
    nh, nl = mesh.shape["high"], mesh.shape["low"]
    n = nh * nl

    def on_device(wave, level, diag, turn):
        blocks, rows, lanes = level.shape
        rp = rows // (n // blocks)
        parts = 2 if rp % 16 == 0 else 1
        hbm = pl.BlockSpec(memory_space=pltpu.HBM)
        dma = pltpu.SemaphoreType.DMA
        return pl.pallas_call(
            functools.partial(kernel, nh, nl, parts),
            out_shape=jax.ShapeDtypeStruct(wave.shape, F32),
            in_specs=[hbm] * 4,
            out_specs=hbm,
            scratch_shapes=[
                pltpu.VMEM(wave.shape, F32),
                dma((blocks // 2,)),
                pltpu.VMEM(diag.shape, F32),
                pltpu.SMEM(turn.shape, F32),
                pltpu.VMEM(wave.shape, F32),
                pltpu.VMEM(level.shape, F32),
                pltpu.VMEM((n, parts, 2 * rp // parts, lanes), F32),
                pltpu.VMEM((n, parts, 2 * rp // parts, lanes), F32),
                pltpu.VMEM((n, rp, lanes), F32),
                pltpu.VMEM((n, 2, rp, lanes), F32),
                pltpu.VMEM((n, 2, rp, lanes), F32),
                pltpu.VMEM((2, 2 * lanes, 2 * lanes), BF16),
                pltpu.VMEM((2, 2 * rows, 2 * rows), BF16),
                dma((4,)), dma((n,)), dma((n,)), dma((parts, n)), dma((parts, n)),
                dma((2, parts, n)), dma((2, parts, n)),
            ],
            compiler_params=pltpu.CompilerParams(
                collective_id=0, has_side_effects=True, vmem_limit_bytes=60 * 2**20),
        )(wave, level, diag, turn)

    in_specs = (P(None, ("high", "low"), None, None), P(("high", "low"), None, None), P(), P())
    return jax.shard_map(
        on_device, mesh=mesh, in_specs=in_specs,
        out_specs=P(None, ("high", "low"), None, None), check_vma=False)
```

profile of v0, /device:TPU:8, one launch (start us, length us, event | category | flops | bytes accessed | tf_op | source)
XLA Modules:
  0.0 128.4 jit_solution(3564936564671864241)
XLA Ops:
  0.0 125.2 %shard_map.46 = f32[2,16,128,128]{3,2,1,0:T(8,128)} custom-call(f32[2,16,128,128]{3,2,1,0:T(8,128)} %wave_hbm.1, f32[16,128,128]{2,1,0:T(8,128)} %level_hbm.1, f32[2,128]{1,0:T(2,128)} %diag_hbm.1, f32[2,4]{1,0:T(2,128)} %turn_hbm.1), custom_call_target="tpu_custom_call" | custom-call | tf_op jit(solution)/shard_map/pallas_call | solution.py:312
  125.2 3.1 %copy.6 = f32[2,16,128,128]{3,2,1,0:T(8,128)} copy(f32[2,16,128,128]{3,2,1,0:T(8,128)} %shard_map.46) | data formatting | bytes 4194304
where the time goes:
time: 130 us; the launch traced here: 128 us
  Pallas kernels  125 us (96%)
  local copies, waits for them, and re-layouts  3.14 us (2%)
    pallas_call x1, Pallas kernels, on_device(): pl.pallas_call(functools.partial(kernel, nh, nl, parts), out_shape=jax.Sh...  125 us
    unnamed x1, local copies, waits for them, and re-layouts  3.14 us

commit v1 on v0

--- a/solution.py
+++ b/solution.py
@@ -84,8 +84,8 @@
     return hi, (x - hi.astype(F32)).astype(BF16)
 
 
-def kernel(nh, nl, parts, wave_hbm, level_hbm, diag_hbm, turn_hbm, out_hbm,
-           out, out_sem, diag, turn, wave, level, abuf, recv, lev, back, home, lane_t, row_t,
+def kernel(nh, nl, parts, wave_hbm, level_hbm, diag_hbm, turn_hbm, out,
+           diag, turn, wave, level, abuf, recv, lev, back, home, lane_t, row_t,
            in_sem, lev_send, lev_recv, to_send, to_recv, ret_send, ret_recv):
     n = nh * nl
     blocks, rows, lanes = level.shape
@@ -264,9 +264,6 @@
     def gather(b, part):
         return jnp.concatenate([home[b * cut + p, part] for p in range(cut)], 0)
 
-    def out_copy(i):
-        pair = pl.ds(2 * i, 2)
-        return pltpu.make_async_copy(out.at[:, pair], out_hbm.at[:, pair], out_sem.at[i])
 
     for part in range(2):
         for q in range(parts):
@@ -283,8 +280,6 @@
                     re = wave[0, at]
                     out[0, at] = jnp.where(odd, x, re) * sign
                     out[1, at] = jnp.where(odd, -re, x) * sign
-            if part == 1:
-                out_copy(i).start()
             return carry
         lax.fori_loop(0, blocks // 2, last, 0, unroll=4)
 
@@ -295,8 +290,19 @@
             for part in range(2):
                 ret_copy(part, q)(d, at).wait_send()
     others(drain)
-    for i in range(blocks // 2):
-        out_copy(i).wait()
+
+
+def put_out(done, out, sem):
+    blocks = done.shape[1]
+    copies = []
+    for part in range(2):
+        for q in range(2):
+            at = pl.ds(q * (blocks // 2), blocks // 2)
+            copies.append(pltpu.make_async_copy(done.at[part, at], out.at[part, at], sem.at[2 * part + q]))
+    for copy in copies:
+        copy.start()
+    for copy in copies:
+        copy.wait()
 
 
 def solution(mesh):
@@ -309,14 +315,12 @@
         parts = 2 if rp % 16 == 0 else 1
         hbm = pl.BlockSpec(memory_space=pltpu.HBM)
         dma = pltpu.SemaphoreType.DMA
-        return pl.pallas_call(
+        done = pl.pallas_call(
             functools.partial(kernel, nh, nl, parts),
-            out_shape=jax.ShapeDtypeStruct(wave.shape, F32),
+            out_shape=pltpu.VMEM(wave.shape, F32),
             in_specs=[hbm] * 4,
-            out_specs=hbm,
+            out_specs=pl.BlockSpec(memory_space=pltpu.VMEM),
             scratch_shapes=[
-                pltpu.VMEM(wave.shape, F32),
-                dma((blocks // 2,)),
                 pltpu.VMEM(diag.shape, F32),
                 pltpu.SMEM(turn.shape, F32),
                 pltpu.VMEM(wave.shape, F32),
@@ -332,8 +336,16 @@
                 dma((2, parts, n)), dma((2, parts, n)),
             ],
             compiler_params=pltpu.CompilerParams(
-                collective_id=0, has_side_effects=True, vmem_limit_bytes=60 * 2**20),
-        )(wave, level, diag, turn)
+                collective_id=0, has_side_effects=True, vmem_limit_bytes=20 * 2**20),
+        )(*[pltpu.with_memory_space_constraint(x, pltpu.HBM) for x in (wave, level, diag, turn)])
+        return pl.pallas_call(
+            put_out,
+            out_shape=jax.ShapeDtypeStruct(wave.shape, F32),
+            in_specs=[pl.BlockSpec(memory_space=pltpu.VMEM)],
+            out_specs=hbm,
+            scratch_shapes=[dma((4,))],
+            compiler_params=pltpu.CompilerParams(vmem_limit_bytes=2**20),
+        )(done)
 
     in_specs = (P(None, ("high", "low"), None, None), P(("high", "low"), None, None), P(), P())
     return jax.shard_map(

time: 130 us -> 128 us (0.985)
  local copies, waits for them, and re-layouts: 3.14 us -> 0 us
    unnamed x1 -> x0, local copies, waits for them, and re-layouts: 3.14 us -> none
    pallas_call x1 -> x2, Pallas kernels: 125 us -> 126 us  [the longest x1 125 us: on_device(): pl.pallas_call(functools.partial(kernel, nh, nl, parts), out_shape=pltpu....]
where the time goes in v1:
time: 128 us; the launch traced here: 126 us
  Pallas kernels  126 us (98%)
    pallas_call x1, Pallas kernels, on_device(): pl.pallas_call(functools.partial(kernel, nh, nl, parts), out_shape=pltpu....  125 us

profile of v1, /device:TPU:8, one launch (start us, length us, event | category | flops | bytes accessed | tf_op | source)
XLA Modules:
  0.0 126.3 jit_solution(2495421250907997754)
XLA Ops:
  0.0 124.9 %shard_map.46.done = f32[2,16,128,128]{3,2,1,0:T(8,128)S(1)} custom-call(f32[2,16,128,128]{3,2,1,0:T(8,128)} %wave_hbm.1, f32[16,128,128]{2,1,0:T(8,128)} %level_hbm.1, f32[2,128]{1,0:T(2,128)} %diag_hbm.1, f32[2,4]{1,0:T(2,128)} %turn_hbm.1), custom_call_target="tpu_custom_call" | custom-call | tf_op jit(solution)/shard_map/pallas_call | solution.py:318
  124.9 1.3 %shard_map.47 = f32[2,16,128,128]{3,2,1,0:T(8,128)} custom-call(f32[2,16,128,128]{3,2,1,0:T(8,128)S(1)} %shard_map.46.done), custom_call_target="tpu_custom_call" | custom-call | tf_op jit(solution)/shard_map/pallas_call | solution.py:341

commit v2 on v1

--- a/solution.py
+++ b/solution.py
@@ -86,7 +86,7 @@
 
 def kernel(nh, nl, parts, wave_hbm, level_hbm, diag_hbm, turn_hbm, out,
            diag, turn, wave, level, abuf, recv, lev, back, home, lane_t, row_t,
-           in_sem, lev_send, lev_recv, to_send, to_recv, ret_send, ret_recv):
+           in_sem, ready, lev_send, lev_recv, to_send, to_recv, ret_send, ret_recv):
     n = nh * nl
     blocks, rows, lanes = level.shape
     cut = n // blocks
@@ -95,55 +95,92 @@
     h, l = lax.axis_index("high"), lax.axis_index("low")
     me = h * nl + l
 
-    def others(body):
+    quad = nl // 4
+    plane = nh * quad
+
+    def others(body, start=0):
         def step(k, carry):
-            dh = lax.rem(h + k // nl, nh)
-            dl = lax.rem(l + k % nl, nl)
+            dh = h ^ (nh - 1 - k % nh)
+            dl = l ^ (nl - 1 - k // nh)
             body(dh * nl + dl, (dh, dl))
             return carry
-        lax.fori_loop(1, n, step, 0)
+        lax.fori_loop(start, n - 1, step, 0)
+
+    def line(body, first):
+        for j in range(first, 4):
+            dl = l ^ (j * quad)
+            body(h * nl + dl, (h, dl))
+
+    def near(body):
+        others(body, n - plane)
+
+    def off_line(body):
+        def step(k, carry):
+            dh = h ^ (nh - 1 - k % (nh - 1))
+            dl = l ^ (nl - 1 - k // (nh - 1))
+            body(dh * nl + dl, (dh, dl))
+            return carry
+        lax.fori_loop(0, nl * (nh - 1), step, 0)
+
+        def column(k, carry):
+            dl = l ^ (k + k // (quad - 1) + 1) if quad > 1 else l
+            body(h * nl + dl, (h, dl))
+            return carry
+        lax.fori_loop(0, 4 * (quad - 1), column, 0)
 
     level_in = pltpu.make_async_copy(level_hbm, level, in_sem.at[0])
     wave_in = pltpu.make_async_copy(wave_hbm, wave, in_sem.at[1])
     diag_in = pltpu.make_async_copy(diag_hbm, diag, in_sem.at[2])
     turn_in = pltpu.make_async_copy(turn_hbm, turn, in_sem.at[3])
+    level_in.start()
     turn_in.start()
     diag_in.start()
-    level_in.start()
     wave_in.start()
 
     barrier = pltpu.get_barrier_semaphore()
-    others(lambda d, at: pl.semaphore_signal(barrier, inc=1, device_id=at, device_id_type=MESH))
-    pl.semaphore_wait(barrier, n - 1)
+
+    def greet(sem):
+        return lambda d, at: pl.semaphore_signal(sem, inc=1, device_id=at, device_id_type=MESH)
+
+    line(greet(barrier), 1)
+    near(greet(barrier))
+    level_in.wait()
+    pl.semaphore_wait(barrier, plane + 2)
 
     def own_rows(d):
         return pl.ds(pl.multiple_of((d % cut) * rp, 8), rp)
 
     def level_copy(d, at):
         return pltpu.make_async_remote_copy(
-            src_ref=level_hbm.at[d // cut, own_rows(d)], dst_ref=lev.at[me],
-            send_sem=lev_send.at[d], recv_sem=lev_recv.at[me],
+            src_ref=level.at[d // cut, own_rows(d)], dst_ref=lev.at[me],
+            send_sem=lev_send, recv_sem=lev_recv,
             device_id=at, device_id_type=MESH)
 
     def to_copy(q):
         return lambda d, at: pltpu.make_async_remote_copy(
-            src_ref=abuf.at[d, q], dst_ref=recv.at[me, q], send_sem=to_send.at[q, d],
-            recv_sem=to_recv.at[q, me], device_id=at, device_id_type=MESH)
+            src_ref=abuf.at[d, q], dst_ref=recv.at[me, q], send_sem=to_send.at[q],
+            recv_sem=to_recv.at[q], device_id=at, device_id_type=MESH)
 
     def ret_copy(part, q):
         part_rows = pl.ds(q * rq, rq)
         return lambda d, at: pltpu.make_async_remote_copy(
             src_ref=back.at[d, part, part_rows], dst_ref=home.at[me, part, part_rows],
-            send_sem=ret_send.at[part, q, d], recv_sem=ret_recv.at[part, q, me],
+            send_sem=ret_send.at[part, q], recv_sem=ret_recv.at[part, q],
             device_id=at, device_id_type=MESH)
 
     def start_all(copy):
         others(lambda d, at: copy(d, at).start())
 
-    def wait_all(block_of, sem):
-        others(lambda d, at: pltpu.make_async_copy(block_of(d), block_of(d), sem.at[d]).wait())
-
-    start_all(level_copy)
+    def wait_all(blocks_of, sem):
+        most = blocks_of(pl.ds(0, n - 1))
+        pltpu.make_async_copy(most, most, sem).wait()
+
+    line(lambda d, at: level_copy(d, at).start(), 2)
+    near(greet(ready))
+    pl.semaphore_wait(ready, plane - 1)
+    dl = l ^ quad
+    level_copy(h * nl + dl, (h, dl)).start()
+    off_line(lambda d, at: level_copy(d, at).start())
 
     turn_in.wait()
     diag_in.wait()
@@ -191,7 +228,6 @@
         k = (ones + (ones_dev + pop(b, bits_of(blocks)))) & 3
         return (k & 1) == 1, jnp.where(k >= 2, -1.0, 1.0)
 
-    level_in.wait()
     wave_in.wait()
     lev[me] = level[me // cut, own_rows(me)]
 
@@ -261,6 +297,10 @@
         start_all(ret_copy(1, q))
     home[me] = back[me]
 
+    wait_all(lambda d: lev.at[d], lev_send)
+    for q in range(parts):
+        wait_all(lambda d: abuf.at[d, q], to_send.at[q])
+
     def gather(b, part):
         return jnp.concatenate([home[b * cut + p, part] for p in range(cut)], 0)
 
@@ -282,14 +322,9 @@
                     out[1, at] = jnp.where(odd, -re, x) * sign
             return carry
         lax.fori_loop(0, blocks // 2, last, 0, unroll=4)
-
-    def drain(d, at):
-        level_copy(d, at).wait_send()
-        for q in range(parts):
-            to_copy(q)(d, at).wait_send()
-            for part in range(2):
-                ret_copy(part, q)(d, at).wait_send()
-    others(drain)
+    for q in range(parts):
+        for part in range(2):
+            wait_all(lambda d: back.at[d, part, pl.ds(q * rq, rq)], ret_send.at[part, q])
 
 
 def put_out(done, out, sem):
@@ -332,8 +367,8 @@
                 pltpu.VMEM((n, 2, rp, lanes), F32),
                 pltpu.VMEM((2, 2 * lanes, 2 * lanes), BF16),
                 pltpu.VMEM((2, 2 * rows, 2 * rows), BF16),
-                dma((4,)), dma((n,)), dma((n,)), dma((parts, n)), dma((parts, n)),
-                dma((2, parts, n)), dma((2, parts, n)),
+                dma((4,)), pltpu.SemaphoreType.REGULAR, dma, dma, dma((parts,)), dma((parts,)),
+                dma((2, parts)), dma((2, parts)),
             ],
             compiler_params=pltpu.CompilerParams(
                 collective_id=0, has_side_effects=True, vmem_limit_bytes=20 * 2**20),

time: 128 us -> 124 us (0.969)
  the two profiles are of different devices: /device:TPU:8 before, /device:TPU:0 now
where the time goes in v2:
time: 124 us
  Pallas kernels  124 us (100%)
    pallas_call x1, Pallas kernels, on_device(): pl.pallas_call(functools.partial(kernel, nh, nl, parts), out_shape=pltpu....  123 us

profile of v2, /device:TPU:0, one launch (start us, length us, event | category | flops | bytes accessed | tf_op | source)
XLA Modules:
  0.0 124.3 jit_solution(15687659863295906669)
XLA Ops:
  0.0 123.0 %shard_map.46.done = f32[2,16,128,128]{3,2,1,0:T(8,128)S(1)} custom-call(f32[2,16,128,128]{3,2,1,0:T(8,128)} %wave_hbm.1, f32[16,128,128]{2,1,0:T(8,128)} %level_hbm.1, f32[2,128]{1,0:T(2,128)} %diag_hbm.1, f32[2,4]{1,0:T(2,128)} %turn_hbm.1), custom_call_target="tpu_custom_call" | custom-call | tf_op jit(solution)/shard_map/pallas_call | solution.py:353
  123.0 1.3 %shard_map.47 = f32[2,16,128,128]{3,2,1,0:T(8,128)} custom-call(f32[2,16,128,128]{3,2,1,0:T(8,128)S(1)} %shard_map.46.done), custom_call_target="tpu_custom_call" | custom-call | tf_op jit(solution)/shard_map/pallas_call | solution.py:376

commit v3 on v2

--- a/solution.py
+++ b/solution.py
@@ -66,14 +66,14 @@
     return xs
 
 
-def rotation(count, c, s, transposed):
+def rotation(count, c, s, transposed, mixed):
     i = lax.broadcasted_iota(jnp.int32, (count, count), 0)
     j = lax.broadcasted_iota(jnp.int32, (count, count), 1)
     if transposed:
         i, j = j, i
     c, s = c[:1, :count], s[:1, :count]
-    table = jnp.ones((count, count), F32)
-    for q in range(bits_of(count)):
+    table = jnp.where((i >> mixed) == (j >> mixed), 1.0, 0.0)
+    for q in range(mixed):
         a, b = (i >> q) & 1, (j >> q) & 1
         table = table * jnp.where(a == b, c, jnp.where(a == 1, s, -s))
     return table
@@ -98,35 +98,44 @@
     quad = nl // 4
     plane = nh * quad
 
-    def others(body, start=0):
+    zi, yi = l // quad, l % quad
+
+    def call(body, dh, dl):
+        body(dh * nl + dl, (dh, dl))
+
+    def far_line(j):
+        return jnp.where(zi < 2, 3 - j, j) * quad
+
+    def far(body):
         def step(k, carry):
-            dh = h ^ (nh - 1 - k % nh)
-            dl = l ^ (nl - 1 - k // nh)
-            body(dh * nl + dl, (dh, dl))
-            return carry
-        lax.fori_loop(start, n - 1, step, 0)
-
-    def line(body, first):
-        for j in range(first, 4):
-            dl = l ^ (j * quad)
-            body(h * nl + dl, (h, dl))
-
-    def near(body):
-        others(body, n - plane)
+            t = k // nh
+            call(body, h ^ (nh - 1 - k % nh), far_line(t // quad) + (yi ^ (quad - 1 - t % quad)))
+            return carry
+        lax.fori_loop(0, n // 2, step, 0)
+
+    def near(body, count=n // 2 - 1):
+        def step(k, carry):
+            call(body, h ^ (nh - 1 - k % nh), l ^ (nl // 2 - 1 - k // nh))
+            return carry
+        lax.fori_loop(n // 2 - 1 - count, n // 2 - 1, step, 0)
+
+    def others(body):
+        near(body)
+        far(body)
 
     def off_line(body):
         def step(k, carry):
-            dh = h ^ (nh - 1 - k % (nh - 1))
-            dl = l ^ (nl - 1 - k // (nh - 1))
-            body(dh * nl + dl, (dh, dl))
-            return carry
-        lax.fori_loop(0, nl * (nh - 1), step, 0)
+            t = k // (nh - 1)
+            call(body, h ^ (nh - 1 - k % (nh - 1)), far_line(t // quad) + (yi ^ (quad - 1 - t % quad)))
+            return carry
+        lax.fori_loop(0, (nh - 1) * 2 * quad, step, 0)
 
         def column(k, carry):
-            dl = l ^ (k + k // (quad - 1) + 1) if quad > 1 else l
-            body(h * nl + dl, (h, dl))
-            return carry
-        lax.fori_loop(0, 4 * (quad - 1), column, 0)
+            t = k // (quad - 1)
+            call(body, h, far_line(t) + (yi ^ (quad - 1 - k % (quad - 1))))
+            return carry
+        if quad > 1:
+            lax.fori_loop(0, 2 * (quad - 1), column, 0)
 
     level_in = pltpu.make_async_copy(level_hbm, level, in_sem.at[0])
     wave_in = pltpu.make_async_copy(wave_hbm, wave, in_sem.at[1])
@@ -142,8 +151,9 @@
     def greet(sem):
         return lambda d, at: pl.semaphore_signal(sem, inc=1, device_id=at, device_id_type=MESH)
 
-    line(greet(barrier), 1)
-    near(greet(barrier))
+    for j in range(1, 4):
+        call(greet(barrier), h, l ^ (j * quad))
+    near(greet(barrier), plane - 1)
     level_in.wait()
     pl.semaphore_wait(barrier, plane + 2)
 
@@ -161,26 +171,31 @@
             src_ref=abuf.at[d, q], dst_ref=recv.at[me, q], send_sem=to_send.at[q],
             recv_sem=to_recv.at[q], device_id=at, device_id_type=MESH)
 
-    def ret_copy(part, q):
-        part_rows = pl.ds(q * rq, rq)
+    pieces = [(q, 0, 2) for q in range(parts - 1)] + [(parts - 1, 0, 1), (parts - 1, 1, 1)]
+
+    def piece_of(buf, d, i):
+        q, part, count = pieces[i]
+        return buf.at[d, q, pl.ds(part, count)]
+
+    def ret_copy(i):
         return lambda d, at: pltpu.make_async_remote_copy(
-            src_ref=back.at[d, part, part_rows], dst_ref=home.at[me, part, part_rows],
-            send_sem=ret_send.at[part, q], recv_sem=ret_recv.at[part, q],
+            src_ref=piece_of(back, d, i), dst_ref=piece_of(home, me, i),
+            send_sem=ret_send.at[i], recv_sem=ret_recv.at[i],
             device_id=at, device_id_type=MESH)
-
-    def start_all(copy):
-        others(lambda d, at: copy(d, at).start())
 
     def wait_all(blocks_of, sem):
         most = blocks_of(pl.ds(0, n - 1))
         pltpu.make_async_copy(most, most, sem).wait()
 
-    line(lambda d, at: level_copy(d, at).start(), 2)
-    near(greet(ready))
+    def start(copy):
+        return lambda d, at: copy(d, at).start()
+
+    for j in range(2):
+        call(start(level_copy), h, far_line(j) + yi)
+    near(greet(ready), plane - 1)
     pl.semaphore_wait(ready, plane - 1)
-    dl = l ^ quad
-    level_copy(h * nl + dl, (h, dl)).start()
-    off_line(lambda d, at: level_copy(d, at).start())
+    off_line(start(level_copy))
+    near(start(level_copy))
 
     turn_in.wait()
     diag_in.wait()
@@ -189,11 +204,11 @@
     for layer in range(2):
         turns.append([cos_sin(jnp.full((8, lanes), turn[layer, g], F32)) for g in range(4)])
         c, s = turns[layer][0]
-        hi, lo = split(rotation(lanes, c, s, True))
+        hi, lo = split(rotation(lanes, c, s, True, bits_of(lanes)))
         lane_t[layer] = jnp.concatenate(
             [jnp.concatenate([hi, lo], 1), jnp.concatenate([hi, jnp.zeros_like(hi)], 1)], 0)
         c, s = turns[layer][1]
-        hi, lo = split(rotation(rows, c, s, False))
+        hi, lo = split(rotation(rows, c, s, False, bits_of(rows if layer == 0 else rq)))
         row_t[layer] = jnp.concatenate(
             [jnp.concatenate([hi, hi], 1), jnp.concatenate([lo, jnp.zeros_like(hi)], 1)], 0)
 
@@ -224,8 +239,8 @@
             return carry
         lax.fori_loop(0, cut * per, body, 0)
 
-    def quarter(b):
-        k = (ones + (ones_dev + pop(b, bits_of(blocks)))) & 3
+    def quarter(count):
+        k = (ones + count) & 3
         return (k & 1) == 1, jnp.where(k >= 2, -1.0, 1.0)
 
     wave_in.wait()
@@ -233,7 +248,7 @@
 
     def first(b, carry):
         c, s = cos_sin(level[b] * diag[pl.ds(0, 1), :])
-        odd, sign = quarter(b)
+        odd, sign = quarter(ones_dev + pop(b, bits_of(blocks)))
         cc = jnp.where(odd, s, c) * sign
         ss = jnp.where(odd, -c, s) * sign
         re, im = wave[0, b], wave[1, b]
@@ -248,7 +263,7 @@
     lax.fori_loop(0, blocks, first, 0)
     for q in range(parts):
         mix_blocks(abuf, q, 0, 2 * rq, 0)
-        start_all(to_copy(q))
+        others(start(to_copy(q)))
         recv[me, q] = abuf[me, q]
 
     def dev_turns(layer):
@@ -271,60 +286,67 @@
                 ys[d] = y * c - x * s
             ys = mix_list(ys, dev_turns(1))
             for d in range(n):
-                back[d, 1, at_part] = ys[d]
+                back[d, q, 1, at] = ys[d]
             xs = mix_list([recv[d, q, at] for d in range(n)], dev_turns(1))
             for d in range(n):
-                back[d, 0, at_part] = xs[d]
+                back[d, q, 0, at] = xs[d]
             return carry
         lax.fori_loop(0, rq // 8, body, 0)
 
-    def middle_lanes(part, q):
-        group = min(n, 256 // rq)
-        at = pl.ds(q * rq, rq)
-        for i in range(n // group):
+    group = rows // rq
+
+    def finish(q):
+        def body(i, carry):
             ds = pl.ds(i * group, group)
-            z = mix_lanes(back[ds, part, at].reshape(group * rq, lanes), 1)
-            back[ds, part, at] = z.reshape(group, rq, lanes)
+            z = [back[ds, q, part].reshape(rows, lanes) for part in range(2)]
+            z = mix_lanes(jnp.concatenate(z, 0), 1)
+            re, im = mix_rows(z[:rows], z[rows:], 1)
+            odd, sign = quarter(pop(i, bits_of(n // group)))
+            back[ds, q, 0] = (jnp.where(odd, im, re) * sign).reshape(group, rq, lanes)
+            back[ds, q, 1] = (jnp.where(odd, -re, im) * sign).reshape(group, rq, lanes)
+            return carry
+        lax.fori_loop(0, n // group, body, 0, unroll=2)
 
     wait_all(lambda d: lev.at[d], lev_recv)
     for q in range(parts):
         wait_all(lambda d: recv.at[d, q], to_recv.at[q])
         middle(q)
-        middle_lanes(0, q)
-        start_all(ret_copy(0, q))
-        middle_lanes(1, q)
-    for q in range(parts):
-        start_all(ret_copy(1, q))
+        finish(q)
+        for i, piece in enumerate(pieces):
+            if piece[0] == q:
+                others(start(ret_copy(i)))
     home[me] = back[me]
 
     wait_all(lambda d: lev.at[d], lev_send)
     for q in range(parts):
         wait_all(lambda d: abuf.at[d, q], to_send.at[q])
 
-    def gather(b, part):
-        return jnp.concatenate([home[b * cut + p, part] for p in range(cut)], 0)
-
-
-    for part in range(2):
-        for q in range(parts):
-            wait_all(lambda d: home.at[d, part, pl.ds(q * rq, rq)], ret_recv.at[part, q])
-            mix_blocks(home, part, q * rq, rq, 1)
-
-        def last(i, carry):
-            b = 2 * i
-            for at, x in zip((b, b + 1), mix_rows(gather(b, part), gather(b + 1, part), 1)):
-                if part == 0:
-                    wave[0, at] = x
-                else:
-                    odd, sign = quarter(at)
-                    re = wave[0, at]
-                    out[0, at] = jnp.where(odd, x, re) * sign
-                    out[1, at] = jnp.where(odd, -re, x) * sign
-            return carry
-        lax.fori_loop(0, blocks // 2, last, 0, unroll=4)
-    for q in range(parts):
-        for part in range(2):
-            wait_all(lambda d: back.at[d, part, pl.ds(q * rq, rq)], ret_send.at[part, q])
+    own_turns = [turns[1][1]] * bits_of(cut) + [turns[1][2]] * bits_of(blocks)
+
+    def settle(q, part):
+        def body(t, carry):
+            at = pl.ds(pl.multiple_of(t * 8, 8), 8)
+            xs = mix_list([home[d, q, part, at] for d in range(n)], own_turns)
+            for d in range(n):
+                if q < parts - 1:
+                    home[d, q, part, at] = xs[d]
+                    continue
+                ys = [home[d, r, part, at] for r in range(q)] + [xs[d]]
+                ys = mix_list(ys, [turns[1][1]] * bits_of(parts))
+                b, p = d // cut, d % cut
+                for r in range(parts):
+                    k = (d.bit_count() + r.bit_count() - part) % 4
+                    y = -ys[r] if k in (1, 2) else ys[r]
+                    out[k % 2, b, pl.ds(pl.multiple_of(p * rp + r * rq + t * 8, 8), 8)] = y
+            return carry
+        lax.fori_loop(0, rq // 8, body, 0)
+
+    for i, (q, part, count) in enumerate(pieces):
+        wait_all(lambda d: piece_of(home, d, i), ret_recv.at[i])
+        for j in range(count):
+            settle(q, part + j)
+    for i in range(len(pieces)):
+        wait_all(lambda d: piece_of(back, d, i), ret_send.at[i])
 
 
 def put_out(done, out, sem):
@@ -363,12 +385,12 @@
                 pltpu.VMEM((n, parts, 2 * rp // parts, lanes), F32),
                 pltpu.VMEM((n, parts, 2 * rp // parts, lanes), F32),
                 pltpu.VMEM((n, rp, lanes), F32),
-                pltpu.VMEM((n, 2, rp, lanes), F32),
-                pltpu.VMEM((n, 2, rp, lanes), F32),
+                pltpu.VMEM((n, parts, 2, rp // parts, lanes), F32),
+                pltpu.VMEM((n, parts, 2, rp // parts, lanes), F32),
                 pltpu.VMEM((2, 2 * lanes, 2 * lanes), BF16),
                 pltpu.VMEM((2, 2 * rows, 2 * rows), BF16),
                 dma((4,)), pltpu.SemaphoreType.REGULAR, dma, dma, dma((parts,)), dma((parts,)),
-                dma((2, parts)), dma((2, parts)),
+                dma((parts + 1,)), dma((parts + 1,)),
             ],
             compiler_params=pltpu.CompilerParams(
                 collective_id=0, has_side_effects=True, vmem_limit_bytes=20 * 2**20),

time: 124 us -> 120 us (0.968)
  the two profiles are of different devices: /device:TPU:0 before, /device:TPU:8 now
where the time goes in v3:
time: 120 us
  Pallas kernels  120 us (100%)
    pallas_call x1, Pallas kernels, on_device(): pl.pallas_call(functools.partial(kernel, nh, nl, parts), out_shape=pltpu....  119 us

profile of v3, /device:TPU:8, one launch (start us, length us, event | category | flops | bytes accessed | tf_op | source)
XLA Modules:
  0.0 119.9 jit_solution(15004328980934328634)
XLA Ops:
  0.0 118.6 %shard_map.46.done = f32[2,16,128,128]{3,2,1,0:T(8,128)S(1)} custom-call(f32[2,16,128,128]{3,2,1,0:T(8,128)} %wave_hbm.1, f32[16,128,128]{2,1,0:T(8,128)} %level_hbm.1, f32[2,128]{1,0:T(2,128)} %diag_hbm.1, f32[2,4]{1,0:T(2,128)} %turn_hbm.1), custom_call_target="tpu_custom_call" | custom-call | tf_op jit(solution)/shard_map/pallas_call | solution.py:375
  118.6 1.3 %shard_map.47 = f32[2,16,128,128]{3,2,1,0:T(8,128)} custom-call(f32[2,16,128,128]{3,2,1,0:T(8,128)S(1)} %shard_map.46.done), custom_call_target="tpu_custom_call" | custom-call | tf_op jit(solution)/shard_map/pallas_call | solution.py:398

commit v4 on v3

--- a/solution.py
+++ b/solution.py
@@ -85,20 +85,24 @@
 
 
 def kernel(nh, nl, parts, wave_hbm, level_hbm, diag_hbm, turn_hbm, out,
-           diag, turn, wave, level, abuf, recv, lev, back, home, lane_t, row_t,
-           in_sem, ready, lev_send, lev_recv, to_send, to_recv, ret_send, ret_recv):
+           diag, turn, wave, level, relay, abuf, recv, lev, back, home, lane_t, row_t,
+           in_sem, ready, relay_send, relay_recv, lev_send, lev_recv, to_send, to_recv, ret_send, ret_recv):
     n = nh * nl
-    blocks, rows, lanes = level.shape
+    rp, lanes = level.shape[-2:]
+    blocks, rows = wave.shape[1:3]
     cut = n // blocks
-    rp = rows // cut
     rq = rp // parts
     h, l = lax.axis_index("high"), lax.axis_index("low")
     me = h * nl + l
 
     quad = nl // 4
-    plane = nh * quad
+    half = nl // 2
 
     zi, yi = l // quad, l % quad
+    side = zi // 2
+    partner = h * nl + (l ^ (3 * quad))
+    directions = [(1 << i, 0) for i in range(bits_of(nh))] + [(0, 1 << i) for i in range(bits_of(quad))]
+    directions += [(0, quad), (0, 3 * quad)]
 
     def call(body, dh, dl):
         body(dh * nl + dl, (dh, dl))
@@ -113,35 +117,24 @@
             return carry
         lax.fori_loop(0, n // 2, step, 0)
 
-    def near(body, count=n // 2 - 1):
+    def near(body):
         def step(k, carry):
-            call(body, h ^ (nh - 1 - k % nh), l ^ (nl // 2 - 1 - k // nh))
-            return carry
-        lax.fori_loop(n // 2 - 1 - count, n // 2 - 1, step, 0)
+            call(body, h ^ (nh - 1 - k % nh), l ^ (half - 1 - k // nh))
+            return carry
+        lax.fori_loop(0, n // 2 - 1, step, 0)
 
     def others(body):
         near(body)
         far(body)
 
-    def off_line(body):
-        def step(k, carry):
-            t = k // (nh - 1)
-            call(body, h ^ (nh - 1 - k % (nh - 1)), far_line(t // quad) + (yi ^ (quad - 1 - t % quad)))
-            return carry
-        lax.fori_loop(0, (nh - 1) * 2 * quad, step, 0)
-
-        def column(k, carry):
-            t = k // (quad - 1)
-            call(body, h, far_line(t) + (yi ^ (quad - 1 - k % (quad - 1))))
-            return carry
-        if quad > 1:
-            lax.fori_loop(0, 2 * (quad - 1), column, 0)
-
-    level_in = pltpu.make_async_copy(level_hbm, level, in_sem.at[0])
+    def level_in(which, i):
+        return pltpu.make_async_copy(level_hbm.at[:, which], level.at[:, which], in_sem.at[i])
+
     wave_in = pltpu.make_async_copy(wave_hbm, wave, in_sem.at[1])
     diag_in = pltpu.make_async_copy(diag_hbm, diag, in_sem.at[2])
     turn_in = pltpu.make_async_copy(turn_hbm, turn, in_sem.at[3])
-    level_in.start()
+    level_in(1 - side, 0).start()
+    level_in(side, 4).start()
     turn_in.start()
     diag_in.start()
     wave_in.start()
@@ -151,18 +144,29 @@
     def greet(sem):
         return lambda d, at: pl.semaphore_signal(sem, inc=1, device_id=at, device_id_type=MESH)
 
-    for j in range(1, 4):
-        call(greet(barrier), h, l ^ (j * quad))
-    near(greet(barrier), plane - 1)
-    level_in.wait()
-    pl.semaphore_wait(barrier, plane + 2)
-
-    def own_rows(d):
-        return pl.ds(pl.multiple_of((d % cut) * rp, 8), rp)
+    for dh, dl in directions:
+        call(greet(barrier), h ^ dh, l ^ dl)
+    level_in(1 - side, 0).wait()
+    pl.semaphore_wait(barrier, len(directions))
+
+    relay_copy = pltpu.make_async_remote_copy(
+        src_ref=level.at[:, 1 - side], dst_ref=relay, send_sem=relay_send, recv_sem=relay_recv,
+        device_id=(h, l ^ (3 * quad)), device_id_type=MESH)
+    relay_copy.start()
+    for i, (dh, dl) in enumerate(directions[1:]):
+        call(greet(ready.at[i]), h ^ dh, l ^ dl)
+        pl.semaphore_wait(ready.at[i], 1)
+    level_in(side, 4).wait()
 
     def level_copy(d, at):
         return pltpu.make_async_remote_copy(
-            src_ref=level.at[d // cut, own_rows(d)], dst_ref=lev.at[me],
+            src_ref=level.at[at[0], side, at[1] % half], dst_ref=lev.at[me],
+            send_sem=lev_send, recv_sem=lev_recv,
+            device_id=at, device_id_type=MESH)
+
+    def pass_copy(d, at):
+        return pltpu.make_async_remote_copy(
+            src_ref=relay.at[at[0], at[1] % half], dst_ref=lev.at[partner],
             send_sem=lev_send, recv_sem=lev_recv,
             device_id=at, device_id_type=MESH)
 
@@ -183,18 +187,13 @@
             send_sem=ret_send.at[i], recv_sem=ret_recv.at[i],
             device_id=at, device_id_type=MESH)
 
-    def wait_all(blocks_of, sem):
-        most = blocks_of(pl.ds(0, n - 1))
+    def wait_all(blocks_of, sem, count=n - 1):
+        most = blocks_of(pl.ds(0, count))
         pltpu.make_async_copy(most, most, sem).wait()
 
     def start(copy):
         return lambda d, at: copy(d, at).start()
 
-    for j in range(2):
-        call(start(level_copy), h, far_line(j) + yi)
-    near(greet(ready), plane - 1)
-    pl.semaphore_wait(ready, plane - 1)
-    off_line(start(level_copy))
     near(start(level_copy))
 
     turn_in.wait()
@@ -244,10 +243,12 @@
         return (k & 1) == 1, jnp.where(k >= 2, -1.0, 1.0)
 
     wave_in.wait()
-    lev[me] = level[me // cut, own_rows(me)]
+    lev[me] = level[h, side, l % half]
 
     def first(b, carry):
-        c, s = cos_sin(level[b] * diag[pl.ds(0, 1), :])
+        slots = [b * cut + p for p in range(cut)]
+        e = jnp.concatenate([level[d // nl, d % nl // half, d % half] for d in slots], 0)
+        c, s = cos_sin(e * diag[pl.ds(0, 1), :])
         odd, sign = quarter(ones_dev + pop(b, bits_of(blocks)))
         cc = jnp.where(odd, s, c) * sign
         ss = jnp.where(odd, -c, s) * sign
@@ -265,6 +266,10 @@
         mix_blocks(abuf, q, 0, 2 * rq, 0)
         others(start(to_copy(q)))
         recv[me, q] = abuf[me, q]
+        if q == 0:
+            relay_copy.wait_recv()
+            near(start(pass_copy))
+            lev[partner] = relay[h, l % half]
 
     def dev_turns(layer):
         return [turns[layer][3]] * bits_of(nl) + [turns[layer][2]] * bits_of(nh)
@@ -307,7 +312,7 @@
             return carry
         lax.fori_loop(0, n // group, body, 0, unroll=2)
 
-    wait_all(lambda d: lev.at[d], lev_recv)
+    wait_all(lambda d: lev.at[d], lev_recv, n - 2)
     for q in range(parts):
         wait_all(lambda d: recv.at[d, q], to_recv.at[q])
         middle(q)
@@ -317,7 +322,8 @@
                 others(start(ret_copy(i)))
     home[me] = back[me]
 
-    wait_all(lambda d: lev.at[d], lev_send)
+    relay_copy.wait_send()
+    wait_all(lambda d: lev.at[d], lev_send, n - 2)
     for q in range(parts):
         wait_all(lambda d: abuf.at[d, q], to_send.at[q])
 
@@ -369,6 +375,7 @@
     def on_device(wave, level, diag, turn):
         blocks, rows, lanes = level.shape
         rp = rows // (n // blocks)
+        level = level.reshape(nh, 2, nl // 2, rp, lanes)
         parts = 2 if rp % 16 == 0 else 1
         hbm = pl.BlockSpec(memory_space=pltpu.HBM)
         dma = pltpu.SemaphoreType.DMA
@@ -382,6 +389,7 @@
                 pltpu.SMEM(turn.shape, F32),
                 pltpu.VMEM(wave.shape, F32),
                 pltpu.VMEM(level.shape, F32),
+                pltpu.VMEM((nh, nl // 2, rp, lanes), F32),
                 pltpu.VMEM((n, parts, 2 * rp // parts, lanes), F32),
                 pltpu.VMEM((n, parts, 2 * rp // parts, lanes), F32),
                 pltpu.VMEM((n, rp, lanes), F32),
@@ -389,7 +397,7 @@
                 pltpu.VMEM((n, parts, 2, rp // parts, lanes), F32),
                 pltpu.VMEM((2, 2 * lanes, 2 * lanes), BF16),
                 pltpu.VMEM((2, 2 * rows, 2 * rows), BF16),
-                dma((4,)), pltpu.SemaphoreType.REGULAR, dma, dma, dma((parts,)), dma((parts,)),
+                dma((5,)), pltpu.SemaphoreType.REGULAR((bits_of(n),)), dma, dma, dma, dma, dma((parts,)), dma((parts,)),
                 dma((parts + 1,)), dma((parts + 1,)),
             ],
             compiler_params=pltpu.CompilerParams(

time: 120 us -> 119 us (level)
  no operation moved by 1% of the time
where the time goes in v4:
time: 119 us
  Pallas kernels  119 us (100%)
    pallas_call x1, Pallas kernels, on_device(): pl.pallas_call(functools.partial(kernel, nh, nl, parts), out_shape=pltpu....  117 us

profile of v4, /device:TPU:8, one launch (start us, length us, event | category | flops | bytes accessed | tf_op | source)
XLA Modules:
  0.0 118.8 jit_solution(15172966698307138103)
XLA Ops:
  0.0 117.4 %shard_map.46.done = f32[2,16,128,128]{3,2,1,0:T(8,128)S(1)} custom-call(f32[2,16,128,128]{3,2,1,0:T(8,128)} %wave_hbm.1, f32[4,2,4,64,128]{4,3,2,1,0:T(8,128)} %bitcast.1, f32[2,128]{1,0:T(2,128)} %diag_hbm.1, f32[2,4]{1,0:T(2,128)} %turn_hbm.1), custom_call_target="tpu_custom_call" | custom-call | tf_op jit(solution)/shard_map/pallas_call | solution.py:382
  117.4 1.3 %shard_map.47 = f32[2,16,128,128]{3,2,1,0:T(8,128)} custom-call(f32[2,16,128,128]{3,2,1,0:T(8,128)S(1)} %shard_map.46.done), custom_call_target="tpu_custom_call" | custom-call | tf_op jit(solution)/shard_map/pallas_call | solution.py:406

commit v5 on v4

--- a/solution.py
+++ b/solution.py
@@ -86,7 +86,7 @@
 
 def kernel(nh, nl, parts, wave_hbm, level_hbm, diag_hbm, turn_hbm, out,
            diag, turn, wave, level, relay, abuf, recv, lev, back, home, lane_t, row_t,
-           in_sem, ready, relay_send, relay_recv, lev_send, lev_recv, to_send, to_recv, ret_send, ret_recv):
+           in_sem, reply, ready, relay_send, relay_recv, lev_send, lev_recv, to_send, to_recv, ret_send, ret_recv):
     n = nh * nl
     rp, lanes = level.shape[-2:]
     blocks, rows = wave.shape[1:3]
@@ -101,8 +101,9 @@
     zi, yi = l // quad, l % quad
     side = zi // 2
     partner = h * nl + (l ^ (3 * quad))
-    directions = [(1 << i, 0) for i in range(bits_of(nh))] + [(0, 1 << i) for i in range(bits_of(quad))]
-    directions += [(0, quad), (0, 3 * quad)]
+    edges = [(1 << i, 0, (h >> i) & 1) for i in range(bits_of(nh))]
+    edges += [(0, 1 << i, (l >> i) & 1) for i in range(bits_of(quad))]
+    edges += [(0, quad, zi % 2)]
 
     def call(body, dh, dl):
         body(dh * nl + dl, (dh, dl))
@@ -126,6 +127,22 @@
     def others(body):
         near(body)
         far(body)
+
+    barrier = pltpu.get_barrier_semaphore()
+
+    def greet(sem):
+        return lambda d, at: pl.semaphore_signal(sem, inc=1, device_id=at, device_id_type=MESH)
+
+    def wait_reply(i):
+        @pl.when(edges[i][2] == 0)
+        def _():
+            pl.semaphore_wait(reply.at[i], 1)
+
+    call(greet(barrier), h, l ^ (3 * quad))
+    for dh, dl, upper in edges:
+        @pl.when(upper == 0)
+        def _():
+            call(greet(barrier), h ^ dh, l ^ dl)
 
     def level_in(which, i):
         return pltpu.make_async_copy(level_hbm.at[:, which], level.at[:, which], in_sem.at[i])
@@ -139,24 +156,23 @@
     diag_in.start()
     wave_in.start()
 
-    barrier = pltpu.get_barrier_semaphore()
-
-    def greet(sem):
-        return lambda d, at: pl.semaphore_signal(sem, inc=1, device_id=at, device_id_type=MESH)
-
-    for dh, dl in directions:
-        call(greet(barrier), h ^ dh, l ^ dl)
-    level_in(1 - side, 0).wait()
-    pl.semaphore_wait(barrier, len(directions))
+    pl.semaphore_wait(barrier, sum(upper for _, _, upper in edges) + 1)
 
     relay_copy = pltpu.make_async_remote_copy(
-        src_ref=level.at[:, 1 - side], dst_ref=relay, send_sem=relay_send, recv_sem=relay_recv,
+        src_ref=level_hbm.at[:, 1 - side], dst_ref=relay, send_sem=relay_send, recv_sem=relay_recv,
         device_id=(h, l ^ (3 * quad)), device_id_type=MESH)
     relay_copy.start()
-    for i, (dh, dl) in enumerate(directions[1:]):
+    for i, (dh, dl, upper) in enumerate(edges):
+        @pl.when(upper == 1)
+        def _():
+            call(greet(reply.at[i]), h ^ dh, l ^ dl)
+    for i in range(len(edges)):
+        wait_reply(i)
+    for i, (dh, dl) in enumerate([edge[:2] for edge in edges[1:]] + [(0, 3 * quad)]):
         call(greet(ready.at[i]), h ^ dh, l ^ dl)
         pl.semaphore_wait(ready.at[i], 1)
     level_in(side, 4).wait()
+    level_in(1 - side, 0).wait()
 
     def level_copy(d, at):
         return pltpu.make_async_remote_copy(
@@ -397,7 +413,7 @@
                 pltpu.VMEM((n, parts, 2, rp // parts, lanes), F32),
                 pltpu.VMEM((2, 2 * lanes, 2 * lanes), BF16),
                 pltpu.VMEM((2, 2 * rows, 2 * rows), BF16),
-                dma((5,)), pltpu.SemaphoreType.REGULAR((bits_of(n),)), dma, dma, dma, dma, dma((parts,)), dma((parts,)),
+                dma((5,)), *[pltpu.SemaphoreType.REGULAR((bits_of(n),))] * 2, dma, dma, dma, dma, dma((parts,)), dma((parts,)),
                 dma((parts + 1,)), dma((parts + 1,)),
             ],
             compiler_params=pltpu.CompilerParams(

time: 119 us -> 119 us (level)
  no operation moved by 1% of the time
where the time goes in v5:
time: 119 us; the launch traced here: 118 us
  Pallas kernels  118 us (99%)
    pallas_call x1, Pallas kernels, on_device(): pl.pallas_call(functools.partial(kernel, nh, nl, parts), out_shape=pltpu....  117 us

profile of v5, /device:TPU:8, one launch (start us, length us, event | category | flops | bytes accessed | tf_op | source)
XLA Modules:
  0.0 118.4 jit_solution(6713523939428534891)
XLA Ops:
  0.0 117.0 %shard_map.46.done = f32[2,16,128,128]{3,2,1,0:T(8,128)S(1)} custom-call(f32[2,16,128,128]{3,2,1,0:T(8,128)} %wave_hbm.1, f32[4,2,4,64,128]{4,3,2,1,0:T(8,128)} %bitcast.1, f32[2,128]{1,0:T(2,128)} %diag_hbm.1, f32[2,4]{1,0:T(2,128)} %turn_hbm.1), custom_call_target="tpu_custom_call" | custom-call | tf_op jit(solution)/shard_map/pallas_call | solution.py:398
  117.0 1.3 %shard_map.47 = f32[2,16,128,128]{3,2,1,0:T(8,128)} custom-call(f32[2,16,128,128]{3,2,1,0:T(8,128)S(1)} %shard_map.46.done), custom_call_target="tpu_custom_call" | custom-call | tf_op jit(solution)/shard_map/pallas_call | solution.py:422

commit v6 on v5

--- a/solution.py
+++ b/solution.py
@@ -66,6 +66,19 @@
     return xs
 
 
+def mix_scaled(xs, tangents):
+    for q, t in enumerate(tangents):
+        step = 1 << q
+        ys = list(xs)
+        for i in range(len(xs)):
+            if not i & step:
+                u, v = xs[i], xs[i + step]
+                ys[i] = u - t * v
+                ys[i + step] = v + t * u
+        xs = ys
+    return xs
+
+
 def rotation(count, c, s, transposed, mixed):
     i = lax.broadcasted_iota(jnp.int32, (count, count), 0)
     j = lax.broadcasted_iota(jnp.int32, (count, count), 1)
@@ -84,8 +97,8 @@
     return hi, (x - hi.astype(F32)).astype(BF16)
 
 
-def kernel(nh, nl, parts, wave_hbm, level_hbm, diag_hbm, turn_hbm, out,
-           diag, turn, wave, level, relay, abuf, recv, lev, back, home, lane_t, row_t,
+def kernel(nh, nl, parts, wave_hbm, level_hbm, diag_hbm, turn_hbm, home, tangent,
+           diag, turn, wave, level, relay, abuf, recv, lev, back, lane_t, row_t,
            in_sem, reply, ready, relay_send, relay_recv, lev_send, lev_recv, to_send, to_recv, ret_send, ret_recv):
     n = nh * nl
     rp, lanes = level.shape[-2:]
@@ -314,6 +327,15 @@
             return carry
         lax.fori_loop(0, rq // 8, body, 0)
 
+    tangents = [turns[1][g][1] / turns[1][g][0] for g in (1, 2)]
+    own_tangents = [tangents[0]] * bits_of(cut) + [tangents[1]] * bits_of(blocks)
+    half_tangents = [tangents[0]] * bits_of(parts)
+    tangent[0], tangent[1] = tangents
+    scale = jnp.ones((1, lanes), F32)
+    for g, count in ((1, bits_of(cut * parts)), (2, bits_of(blocks))):
+        for _ in range(count):
+            scale = scale * turns[1][g][0][:1]
+
     group = rows // rq
 
     def finish(q):
@@ -323,6 +345,7 @@
             z = mix_lanes(jnp.concatenate(z, 0), 1)
             re, im = mix_rows(z[:rows], z[rows:], 1)
             odd, sign = quarter(pop(i, bits_of(n // group)))
+            sign = sign * scale
             back[ds, q, 0] = (jnp.where(odd, im, re) * sign).reshape(group, rq, lanes)
             back[ds, q, 1] = (jnp.where(odd, -re, im) * sign).reshape(group, rq, lanes)
             return carry
@@ -343,45 +366,62 @@
     for q in range(parts):
         wait_all(lambda d: abuf.at[d, q], to_send.at[q])
 
-    own_turns = [turns[1][1]] * bits_of(cut) + [turns[1][2]] * bits_of(blocks)
-
     def settle(q, part):
         def body(t, carry):
             at = pl.ds(pl.multiple_of(t * 8, 8), 8)
-            xs = mix_list([home[d, q, part, at] for d in range(n)], own_turns)
+            xs = mix_scaled([home[d, q, part, at] for d in range(n)], own_tangents)
             for d in range(n):
                 if q < parts - 1:
                     home[d, q, part, at] = xs[d]
                     continue
                 ys = [home[d, r, part, at] for r in range(q)] + [xs[d]]
-                ys = mix_list(ys, [turns[1][1]] * bits_of(parts))
-                b, p = d // cut, d % cut
+                ys = mix_scaled(ys, half_tangents)
                 for r in range(parts):
-                    k = (d.bit_count() + r.bit_count() - part) % 4
-                    y = -ys[r] if k in (1, 2) else ys[r]
-                    out[k % 2, b, pl.ds(pl.multiple_of(p * rp + r * rq + t * 8, 8), 8)] = y
+                    home[d, r, part, at] = -ys[r] if place(d, r, part)[1] else ys[r]
             return carry
         lax.fori_loop(0, rq // 8, body, 0)
 
     for i, (q, part, count) in enumerate(pieces):
         wait_all(lambda d: piece_of(home, d, i), ret_recv.at[i])
         for j in range(count):
-            settle(q, part + j)
+            if (q, part) != pieces[-1][:2]:
+                settle(q, part + j)
     for i in range(len(pieces)):
         wait_all(lambda d: piece_of(back, d, i), ret_send.at[i])
 
 
-def put_out(done, out, sem):
-    blocks = done.shape[1]
-    copies = []
-    for part in range(2):
-        for q in range(2):
-            at = pl.ds(q * (blocks // 2), blocks // 2)
-            copies.append(pltpu.make_async_copy(done.at[part, at], out.at[part, at], sem.at[2 * part + q]))
-    for copy in copies:
-        copy.start()
-    for copy in copies:
-        copy.wait()
+def place(d, r, part):
+    k = (d.bit_count() + r.bit_count() - part) % 4
+    return k % 2, k in (1, 2)
+
+
+def close(home, tangent, out_hbm, out, sem):
+    n, parts, _, rq, lanes = home.shape
+    blocks = out.shape[1]
+    cut = n // blocks
+    own_tangents = [tangent[0]] * bits_of(cut) + [tangent[1]] * bits_of(blocks)
+
+    def out_copy(t):
+        at = pl.ds(pl.multiple_of(t * 8, 8), 8)
+        return pltpu.make_async_copy(
+            out.at[:, :, :, :, at], out_hbm.at[:, :, :, :, at], sem.at[t])
+
+    def body(t, carry):
+        at = pl.ds(pl.multiple_of(t * 8, 8), 8)
+        xs = mix_scaled([home[d, parts - 1, 1, at] for d in range(n)], own_tangents)
+        for d in range(n):
+            b, p = d // cut, d % cut
+            ys = [home[d, r, 1, at] for r in range(parts - 1)] + [xs[d]]
+            ys = mix_scaled(ys, [tangent[0]] * bits_of(parts))
+            for r in range(parts):
+                index, minus = place(d, r, 1)
+                out[index, b, p, r, at] = -ys[r] if minus else ys[r]
+                out[1 - index, b, p, r, at] = home[d, r, 0, at]
+        out_copy(t).start()
+        return carry
+    lax.fori_loop(0, rq // 8, body, 0)
+    for t in range(rq // 8):
+        out_copy(t).wait()
 
 
 def solution(mesh):
@@ -394,12 +434,13 @@
         level = level.reshape(nh, 2, nl // 2, rp, lanes)
         parts = 2 if rp % 16 == 0 else 1
         hbm = pl.BlockSpec(memory_space=pltpu.HBM)
+        vmem = pl.BlockSpec(memory_space=pltpu.VMEM)
         dma = pltpu.SemaphoreType.DMA
-        done = pl.pallas_call(
+        home, tangent = pl.pallas_call(
             functools.partial(kernel, nh, nl, parts),
-            out_shape=pltpu.VMEM(wave.shape, F32),
+            out_shape=(pltpu.VMEM((n, parts, 2, rp // parts, lanes), F32), pltpu.VMEM((2, 8, lanes), F32)),
             in_specs=[hbm] * 4,
-            out_specs=pl.BlockSpec(memory_space=pltpu.VMEM),
+            out_specs=(vmem, vmem),
             scratch_shapes=[
                 pltpu.VMEM(diag.shape, F32),
                 pltpu.SMEM(turn.shape, F32),
@@ -410,7 +451,6 @@
                 pltpu.VMEM((n, parts, 2 * rp // parts, lanes), F32),
                 pltpu.VMEM((n, rp, lanes), F32),
                 pltpu.VMEM((n, parts, 2, rp // parts, lanes), F32),
-                pltpu.VMEM((n, parts, 2, rp // parts, lanes), F32),
                 pltpu.VMEM((2, 2 * lanes, 2 * lanes), BF16),
                 pltpu.VMEM((2, 2 * rows, 2 * rows), BF16),
                 dma((5,)), *[pltpu.SemaphoreType.REGULAR((bits_of(n),))] * 2, dma, dma, dma, dma, dma((parts,)), dma((parts,)),
@@ -419,14 +459,16 @@
             compiler_params=pltpu.CompilerParams(
                 collective_id=0, has_side_effects=True, vmem_limit_bytes=20 * 2**20),
         )(*[pltpu.with_memory_space_constraint(x, pltpu.HBM) for x in (wave, level, diag, turn)])
-        return pl.pallas_call(
-            put_out,
-            out_shape=jax.ShapeDtypeStruct(wave.shape, F32),
-            in_specs=[pl.BlockSpec(memory_space=pltpu.VMEM)],
+        split_shape = (2, blocks, n // blocks, parts, rp // parts, lanes)
+        out = pl.pallas_call(
+            close,
+            out_shape=jax.ShapeDtypeStruct(split_shape, F32),
+            in_specs=[vmem, vmem],
             out_specs=hbm,
-            scratch_shapes=[dma((4,))],
-            compiler_params=pltpu.CompilerParams(vmem_limit_bytes=2**20),
-        )(done)
+            scratch_shapes=[pltpu.VMEM(split_shape, F32), dma((rp // parts // 8,))],
+            compiler_params=pltpu.CompilerParams(vmem_limit_bytes=8 * 2**20),
+        )(home, tangent)
+        return out.reshape(wave.shape)
 
     in_specs = (P(None, ("high", "low"), None, None), P(("high", "low"), None, None), P(), P())
     return jax.shard_map(

time: 119 us -> 118 us (level)
  no operation moved by 1% of the time
where the time goes in v6:
time: 118 us
  Pallas kernels  118 us (100%)
    pallas_call x1, Pallas kernels, on_device(): pl.pallas_call(functools.partial(kernel, nh, nl, parts), out_shape=(pltpu...  116 us

profile of v6, /device:TPU:8, one launch (start us, length us, event | category | flops | bytes accessed | tf_op | source)
XLA Modules:
  0.0 118.0 jit_solution(12644642299003230894)
XLA Ops:
  0.0 116.5 %shard_map.46 = (f32[32,2,2,32,128]{4,3,2,1,0:T(8,128)S(1)}, f32[2,8,128]{2,1,0:T(8,128)S(1)}) custom-call(f32[2,16,128,128]{3,2,1,0:T(8,128)} %wave_hbm.1, f32[4,2,4,64,128]{4,3,2,1,0:T(8,128)} %bitcast.2, f32[2,128]{1,0:T(2,128)} %diag_hbm.1, f32[2,4]{1,0:T(2,128)} %turn_hbm.1), custom_call_target="tpu_custom_call" | custom-call | tf_op jit(solution)/shard_map/pallas_call | solution.py:439
  116.5 1.5 %shard_map.47 = f32[2,16,2,2,32,128]{5,4,3,2,1,0:T(8,128)} custom-call(f32[32,2,2,32,128]{4,3,2,1,0:T(8,128)S(1)} %get-tuple-element.7.home, f32[2,8,128]{2,1,0:T(8,128)S(1)} %get-tuple-element.8.tangent), custom_call_target="tpu_custom_call" | custom-call | tf_op jit(solution)/shard_map/pallas_call | solution.py:463

commit v7 on v6

--- a/solution.py
+++ b/solution.py
@@ -153,7 +153,7 @@
 
     call(greet(barrier), h, l ^ (3 * quad))
     for dh, dl, upper in edges:
-        @pl.when(upper == 0)
+        @pl.when(upper + side == 0)
         def _():
             call(greet(barrier), h ^ dh, l ^ dl)
 
@@ -163,27 +163,35 @@
     wave_in = pltpu.make_async_copy(wave_hbm, wave, in_sem.at[1])
     diag_in = pltpu.make_async_copy(diag_hbm, diag, in_sem.at[2])
     turn_in = pltpu.make_async_copy(turn_hbm, turn, in_sem.at[3])
+    pl.semaphore_wait(barrier, (1 - side) * sum(upper for _, _, upper in edges) + 1)
+
+    relay_copy = pltpu.make_async_remote_copy(
+        src_ref=level_hbm.at[:, 1 - side], dst_ref=relay, send_sem=relay_send, recv_sem=relay_recv,
+        device_id=(h, l ^ (3 * quad)), device_id_type=MESH)
+    relay_copy.start()
     level_in(1 - side, 0).start()
     level_in(side, 4).start()
     turn_in.start()
     diag_in.start()
     wave_in.start()
 
-    pl.semaphore_wait(barrier, sum(upper for _, _, upper in edges) + 1)
-
-    relay_copy = pltpu.make_async_remote_copy(
-        src_ref=level_hbm.at[:, 1 - side], dst_ref=relay, send_sem=relay_send, recv_sem=relay_recv,
-        device_id=(h, l ^ (3 * quad)), device_id_type=MESH)
-    relay_copy.start()
-    for i, (dh, dl, upper) in enumerate(edges):
-        @pl.when(upper == 1)
-        def _():
-            call(greet(reply.at[i]), h ^ dh, l ^ dl)
-    for i in range(len(edges)):
-        wait_reply(i)
-    for i, (dh, dl) in enumerate([edge[:2] for edge in edges[1:]] + [(0, 3 * quad)]):
-        call(greet(ready.at[i]), h ^ dh, l ^ dl)
-        pl.semaphore_wait(ready.at[i], 1)
+    @pl.when(side == 0)
+    def _():
+        for i, (dh, dl, upper) in enumerate(edges):
+            @pl.when(upper == 1)
+            def _():
+                call(greet(reply.at[i]), h ^ dh, l ^ dl)
+        for i in range(len(edges)):
+            wait_reply(i)
+        for i, (dh, dl, _) in enumerate(edges):
+            call(greet(ready.at[i]), h ^ dh, l ^ dl)
+            pl.semaphore_wait(ready.at[i], 1)
+        call(greet(ready.at[len(edges)]), h, l ^ (3 * quad))
+
+    @pl.when(side == 1)
+    def _():
+        pl.semaphore_wait(ready.at[len(edges)], 1)
+
     level_in(side, 4).wait()
     level_in(1 - side, 0).wait()
 
@@ -204,16 +212,10 @@
             src_ref=abuf.at[d, q], dst_ref=recv.at[me, q], send_sem=to_send.at[q],
             recv_sem=to_recv.at[q], device_id=at, device_id_type=MESH)
 
-    pieces = [(q, 0, 2) for q in range(parts - 1)] + [(parts - 1, 0, 1), (parts - 1, 1, 1)]
-
-    def piece_of(buf, d, i):
-        q, part, count = pieces[i]
-        return buf.at[d, q, pl.ds(part, count)]
-
-    def ret_copy(i):
+    def ret_copy(q):
         return lambda d, at: pltpu.make_async_remote_copy(
-            src_ref=piece_of(back, d, i), dst_ref=piece_of(home, me, i),
-            send_sem=ret_send.at[i], recv_sem=ret_recv.at[i],
+            src_ref=back.at[d, q], dst_ref=home.at[me, q],
+            send_sem=ret_send.at[q], recv_sem=ret_recv.at[q],
             device_id=at, device_id_type=MESH)
 
     def wait_all(blocks_of, sem, count=n - 1):
@@ -329,7 +331,6 @@
 
     tangents = [turns[1][g][1] / turns[1][g][0] for g in (1, 2)]
     own_tangents = [tangents[0]] * bits_of(cut) + [tangents[1]] * bits_of(blocks)
-    half_tangents = [tangents[0]] * bits_of(parts)
     tangent[0], tangent[1] = tangents
     scale = jnp.ones((1, lanes), F32)
     for g, count in ((1, bits_of(cut * parts)), (2, bits_of(blocks))):
@@ -356,9 +357,7 @@
         wait_all(lambda d: recv.at[d, q], to_recv.at[q])
         middle(q)
         finish(q)
-        for i, piece in enumerate(pieces):
-            if piece[0] == q:
-                others(start(ret_copy(i)))
+        others(start(ret_copy(q)))
     home[me] = back[me]
 
     relay_copy.wait_send()
@@ -366,28 +365,22 @@
     for q in range(parts):
         wait_all(lambda d: abuf.at[d, q], to_send.at[q])
 
-    def settle(q, part):
+    def settle(q):
         def body(t, carry):
             at = pl.ds(pl.multiple_of(t * 8, 8), 8)
-            xs = mix_scaled([home[d, q, part, at] for d in range(n)], own_tangents)
-            for d in range(n):
-                if q < parts - 1:
+            for part in range(2):
+                xs = mix_scaled([home[d, q, part, at] for d in range(n)], own_tangents)
+                for d in range(n):
                     home[d, q, part, at] = xs[d]
-                    continue
-                ys = [home[d, r, part, at] for r in range(q)] + [xs[d]]
-                ys = mix_scaled(ys, half_tangents)
-                for r in range(parts):
-                    home[d, r, part, at] = -ys[r] if place(d, r, part)[1] else ys[r]
             return carry
         lax.fori_loop(0, rq // 8, body, 0)
 
-    for i, (q, part, count) in enumerate(pieces):
-        wait_all(lambda d: piece_of(home, d, i), ret_recv.at[i])
-        for j in range(count):
-            if (q, part) != pieces[-1][:2]:
-                settle(q, part + j)
-    for i in range(len(pieces)):
-        wait_all(lambda d: piece_of(back, d, i), ret_send.at[i])
+    for q in range(parts):
+        wait_all(lambda d: home.at[d, q], ret_recv.at[q])
+        if q < parts - 1:
+            settle(q)
+    for q in range(parts):
+        wait_all(lambda d: back.at[d, q], ret_send.at[q])
 
 
 def place(d, r, part):
@@ -408,15 +401,15 @@
 
     def body(t, carry):
         at = pl.ds(pl.multiple_of(t * 8, 8), 8)
-        xs = mix_scaled([home[d, parts - 1, 1, at] for d in range(n)], own_tangents)
-        for d in range(n):
-            b, p = d // cut, d % cut
-            ys = [home[d, r, 1, at] for r in range(parts - 1)] + [xs[d]]
-            ys = mix_scaled(ys, [tangent[0]] * bits_of(parts))
-            for r in range(parts):
-                index, minus = place(d, r, 1)
-                out[index, b, p, r, at] = -ys[r] if minus else ys[r]
-                out[1 - index, b, p, r, at] = home[d, r, 0, at]
+        for part in range(2):
+            xs = mix_scaled([home[d, parts - 1, part, at] for d in range(n)], own_tangents)
+            for d in range(n):
+                b, p = d // cut, d % cut
+                ys = [home[d, r, part, at] for r in range(parts - 1)] + [xs[d]]
+                ys = mix_scaled(ys, [tangent[0]] * bits_of(parts))
+                for r in range(parts):
+                    index, minus = place(d, r, part)
+                    out[index, b, p, r, at] = -ys[r] if minus else ys[r]
         out_copy(t).start()
         return carry
     lax.fori_loop(0, rq // 8, body, 0)
@@ -454,7 +447,7 @@
                 pltpu.VMEM((2, 2 * lanes, 2 * lanes), BF16),
                 pltpu.VMEM((2, 2 * rows, 2 * rows), BF16),
                 dma((5,)), *[pltpu.SemaphoreType.REGULAR((bits_of(n),))] * 2, dma, dma, dma, dma, dma((parts,)), dma((parts,)),
-                dma((parts + 1,)), dma((parts + 1,)),
+                dma((parts,)), dma((parts,)),
             ],
             compiler_params=pltpu.CompilerParams(
                 collective_id=0, has_side_effects=True, vmem_limit_bytes=20 * 2**20),

time: 118 us -> 117 us (level)
  no operation moved by 1% of the time
where the time goes in v7:
time: 117 us
  Pallas kernels  117 us (100%)
    pallas_call x1, Pallas kernels, on_device(): pl.pallas_call(functools.partial(kernel, nh, nl, parts), out_shape=(pltpu...  116 us

profile of v7, /device:TPU:8, one launch (start us, length us, event | category | flops | bytes accessed | tf_op | source)
XLA Modules:
  0.0 117.1 jit_solution(12768919377101541224)
XLA Ops:
  0.0 115.6 %shard_map.46 = (f32[32,2,2,32,128]{4,3,2,1,0:T(8,128)S(1)}, f32[2,8,128]{2,1,0:T(8,128)S(1)}) custom-call(f32[2,16,128,128]{3,2,1,0:T(8,128)} %wave_hbm.1, f32[4,2,4,64,128]{4,3,2,1,0:T(8,128)} %bitcast.2, f32[2,128]{1,0:T(2,128)} %diag_hbm.1, f32[2,4]{1,0:T(2,128)} %turn_hbm.1), custom_call_target="tpu_custom_call" | custom-call | tf_op jit(solution)/shard_map/pallas_call | solution.py:432
  115.6 1.5 %shard_map.47 = f32[2,16,2,2,32,128]{5,4,3,2,1,0:T(8,128)} custom-call(f32[32,2,2,32,128]{4,3,2,1,0:T(8,128)S(1)} %get-tuple-element.7.home, f32[2,8,128]{2,1,0:T(8,128)S(1)} %get-tuple-element.8.tangent), custom_call_target="tpu_custom_call" | custom-call | tf_op jit(solution)/shard_map/pallas_call | solution.py:456

commit v8 on v7

--- a/solution.py
+++ b/solution.py
@@ -138,8 +138,8 @@
         lax.fori_loop(0, n // 2 - 1, step, 0)
 
     def others(body):
+        far(body)
         near(body)
-        far(body)
 
     barrier = pltpu.get_barrier_semaphore()
 

time: 117 us -> 117 us (level)
  no operation moved by 1% of the time
where the time goes in v8:
time: 117 us
  Pallas kernels  117 us (100%)
    pallas_call x1, Pallas kernels, on_device(): pl.pallas_call(functools.partial(kernel, nh, nl, parts), out_shape=(pltpu...  116 us

profile of v8, /device:TPU:8, one launch (start us, length us, event | category | flops | bytes accessed | tf_op | source)
XLA Modules:
  0.0 117.1 jit_solution(1989527917459659123)
XLA Ops:
  0.0 115.5 %shard_map.46 = (f32[32,2,2,32,128]{4,3,2,1,0:T(8,128)S(1)}, f32[2,8,128]{2,1,0:T(8,128)S(1)}) custom-call(f32[2,16,128,128]{3,2,1,0:T(8,128)} %wave_hbm.1, f32[4,2,4,64,128]{4,3,2,1,0:T(8,128)} %bitcast.2, f32[2,128]{1,0:T(2,128)} %diag_hbm.1, f32[2,4]{1,0:T(2,128)} %turn_hbm.1), custom_call_target="tpu_custom_call" | custom-call | tf_op jit(solution)/shard_map/pallas_call | solution.py:432
  115.6 1.5 %shard_map.47 = f32[2,16,2,2,32,128]{5,4,3,2,1,0:T(8,128)} custom-call(f32[32,2,2,32,128]{4,3,2,1,0:T(8,128)S(1)} %get-tuple-element.7.home, f32[2,8,128]{2,1,0:T(8,128)S(1)} %get-tuple-element.8.tangent), custom_call_target="tpu_custom_call" | custom-call | tf_op jit(solution)/shard_map/pallas_call | solution.py:456

commit v9 on v7

--- a/solution.py
+++ b/solution.py
@@ -163,13 +163,29 @@
     wave_in = pltpu.make_async_copy(wave_hbm, wave, in_sem.at[1])
     diag_in = pltpu.make_async_copy(diag_hbm, diag, in_sem.at[2])
     turn_in = pltpu.make_async_copy(turn_hbm, turn, in_sem.at[3])
+    @pl.when(side == 0)
+    def _():
+        level_in(1 - side, 0).start()
+
     pl.semaphore_wait(barrier, (1 - side) * sum(upper for _, _, upper in edges) + 1)
 
-    relay_copy = pltpu.make_async_remote_copy(
-        src_ref=level_hbm.at[:, 1 - side], dst_ref=relay, send_sem=relay_send, recv_sem=relay_recv,
-        device_id=(h, l ^ (3 * quad)), device_id_type=MESH)
-    relay_copy.start()
-    level_in(1 - side, 0).start()
+    def relay_from(table):
+        return pltpu.make_async_remote_copy(
+            src_ref=table.at[:, 1 - side], dst_ref=relay, send_sem=relay_send, recv_sem=relay_recv,
+            device_id=(h, l ^ (3 * quad)), device_id_type=MESH)
+
+    relay_copy = relay_from(level_hbm)
+
+    @pl.when(side == 0)
+    def _():
+        level_in(1 - side, 0).wait()
+        relay_from(level).start()
+
+    @pl.when(side == 1)
+    def _():
+        relay_copy.start()
+        level_in(1 - side, 0).start()
+
     level_in(side, 4).start()
     turn_in.start()
     diag_in.start()
@@ -193,7 +209,10 @@
         pl.semaphore_wait(ready.at[len(edges)], 1)
 
     level_in(side, 4).wait()
-    level_in(1 - side, 0).wait()
+
+    @pl.when(side == 1)
+    def _():
+        level_in(1 - side, 0).wait()
 
     def level_copy(d, at):
         return pltpu.make_async_remote_copy(

time: 117 us -> 117 us (level)
  no operation moved by 1% of the time
where the time goes in v9:
time: 117 us
  Pallas kernels  117 us (100%)
    pallas_call x1, Pallas kernels, on_device(): pl.pallas_call(functools.partial(kernel, nh, nl, parts), out_shape=(pltpu...  116 us

profile of v9, /device:TPU:8, one launch (start us, length us, event | category | flops | bytes accessed | tf_op | source)
XLA Modules:
  0.0 117.1 jit_solution(8752780644761420609)
XLA Ops:
  0.0 115.6 %shard_map.46 = (f32[32,2,2,32,128]{4,3,2,1,0:T(8,128)S(1)}, f32[2,8,128]{2,1,0:T(8,128)S(1)}) custom-call(f32[2,16,128,128]{3,2,1,0:T(8,128)} %wave_hbm.1, f32[4,2,4,64,128]{4,3,2,1,0:T(8,128)} %bitcast.2, f32[2,128]{1,0:T(2,128)} %diag_hbm.1, f32[2,4]{1,0:T(2,128)} %turn_hbm.1), custom_call_target="tpu_custom_call" | custom-call | tf_op jit(solution)/shard_map/pallas_call | solution.py:451
  115.6 1.5 %shard_map.47 = f32[2,16,2,2,32,128]{5,4,3,2,1,0:T(8,128)} custom-call(f32[32,2,2,32,128]{4,3,2,1,0:T(8,128)S(1)} %get-tuple-element.7.home, f32[2,8,128]{2,1,0:T(8,128)S(1)} %get-tuple-element.8.tangent), custom_call_target="tpu_custom_call" | custom-call | tf_op jit(solution)/shard_map/pallas_call | solution.py:475
